TPU v7x, 32 devices: a whole 2x2x4 slice. The times are simulated.
32 devices in a mesh: grp: 2 (over x), trn: 8 (over z, y), tst: 2 (over core).
Axes of the slice: x: 2, y: 2, z: 4, core: 2. Of those that a mesh axis runs over, the one named last changes fastest.
Arguments:
- test_points: bfloat16 [64, 8192], P(None, ('grp', 'tst')), parts along dimension 1, may hold values from -9 to 9
- train_points: bfloat16 [64, 65536], P(None, ('grp', 'trn')), parts along dimension 1, may hold values from -6 to 6
- weights: bfloat16 [65536], P(('grp', 'trn')), parts along dimension 0, may hold values from -6 to 6
- factor: bfloat16 [65536, 512], P(('grp', 'trn')), parts along dimension 0, may hold values from -1.14904852 to 1.14904852
Outputs:
- mean: float32 [8192], P(('grp', 'tst')), parts along dimension 0
- variance: float32 [8192], P(('grp', 'tst')), parts along dimension 0
There are 2 independent parts, one for each index of `grp`. A program takes and returns all parts, laid end to end along the dimension named above; each array names one. Nothing has to cross between parts.
All inputs are finite; a program needn't handle non-finite values.
Results may differ from a plain program's by a relative error of at most 0.0033.
Values sent between devices are 32-bit elements; how exact they have to be, the bound alone decides.
A program may use at most 64 MiB of HBM per device.

v0:
```python
import functools
import math

import jax
import jax.numpy as jnp
from jax import lax
from jax.experimental import pallas as pl
from jax.experimental.pallas import tpu as pltpu
from jax.sharding import PartitionSpec as P

LOG2E = 1.4426950408889634
STEPS = 16
SHARE = 4
CHUNK = 1024
LINE = 4
LAG_Y = 3
LAG_B = (0, 3, 5, 7)
LAG_A = (0, 7, 9, 11)
LAG_X = 11


def pieces(value):
    high = value.astype(jnp.bfloat16).astype(jnp.float32)
    rest = value - high
    middle = rest.astype(jnp.bfloat16).astype(jnp.float32)
    low = (rest - middle).astype(jnp.bfloat16).astype(jnp.float32)
    return high, middle, low


def pick(row, table, default):
    value = default
    for index, entry in table:
        value = jnp.where(row == index, entry, value)
    return value


def kernel(
    test_ref, train_ref, weights_ref, factor_hbm, out_ref,
    test_aug, train_aug, wide, part, got_y, got_br, got_bl, got_ar, got_al, got_x,
    mean_acc, var_acc, mean_box, var_box,
    s_y, r_y, s_br, r_br, s_bl, r_bl, s_ar, r_ar, s_al, r_al, s_x, r_x,
    s_mean, r_mean, s_var, r_var, factor_ref, factor_sem,
):
    count = mean_box.shape[0]
    pair = count // LINE
    last = LINE - 1
    me = lax.axis_index("trn")
    z = me // pair
    y = me % pair
    dim, rows = test_ref.shape
    local = train_ref.shape[1]
    depth = test_aug.shape[1]
    quarter = rows // (4 * STEPS)
    gb = quarter * SHARE // 8
    ga = quarter - gb
    span = rows // 4
    other = z * pair + (1 - y)
    up, down = me + pair, me - pair

    barrier = pltpu.get_barrier_semaphore()

    def greet(device):
        pl.semaphore_signal(barrier, inc=1, device_id={"trn": device})

    greet(other)
    pl.when(z < last)(lambda: greet(up))
    pl.when(z > 0)(lambda: greet(down))

    fetch = pltpu.make_async_copy(factor_hbm, factor_ref, factor_sem)
    fetch.start()

    def prepare_train(index, carry):
        cols = pl.ds(pl.multiple_of(index * 512, 512), 512)
        points = train_ref[:, cols]
        squares = points.astype(jnp.float32) ** 2
        norm = jnp.sum(squares, axis=0, keepdims=True) * (-4.0 / dim)
        high, middle, low = pieces(norm)
        row = lax.broadcasted_iota(jnp.int32, (16, 512), 0)
        one = jnp.float32(1.0)
        extra = pick(row, ((0, one), (1, one), (2, one), (3, high), (4, middle), (5, low)), jnp.float32(0.0))
        train_aug[:dim, cols] = points
        train_aug[dim : dim + 16, cols] = extra.astype(jnp.bfloat16)
        train_aug[dim + 16 :, cols] = jnp.zeros((depth - dim - 16, 512), jnp.bfloat16)
        return carry

    lax.fori_loop(0, local // 512, prepare_train, 0)
    wide[...] = weights_ref[...].astype(jnp.float32)

    def prepare_test(index, carry):
        cols = pl.ds(pl.multiple_of(index * 256, 256), 256)
        points = test_ref[:, cols].astype(jnp.float32)
        norm = jnp.sum(points * points, axis=0, keepdims=True) * (-4.0 / dim)
        high, middle, low = pieces(norm)
        row = lax.broadcasted_iota(jnp.int32, (8, 256), 0)
        one = jnp.float32(1.0)
        extra = pick(row, ((0, high), (1, middle), (2, low), (3, one), (4, one), (5, one)), jnp.float32(0.0))
        whole = jnp.concatenate(
            [points * (8.0 / dim), extra, jnp.zeros((depth - dim - 8, 256), jnp.float32)], axis=0
        )
        test_aug[cols, :] = whole.T
        return carry

    lax.fori_loop(0, rows // 256, prepare_test, 0)

    def row_of(owner, kind, step):
        inner = gb * STEPS + step * ga if kind else step * gb
        return pl.multiple_of(owner * span + inner, 8)

    def places(step):
        return (
            row_of(2, 0, step), row_of(3, 0, step), row_of(0, 0, step), row_of(1, 0, step),
            row_of(1 - y, 1, step), row_of(3 - y, 1, step), row_of(y, 1, step), row_of(2 + y, 1, step),
        )

    def compute(step):
        where = places(step)
        sizes = (gb,) * 4 + (ga,) * 4
        left = jnp.concatenate(
            [test_aug[pl.ds(at, size), :] for at, size in zip(where, sizes)], axis=0
        ).astype(jnp.bfloat16)
        total = None
        means = None
        for begin in range(0, local, CHUNK):
            power = jnp.dot(
                left, train_aug[:, begin : begin + CHUNK], preferred_element_type=jnp.float32
            )
            values = jnp.exp2(power * LOG2E).astype(jnp.bfloat16)
            scaled = values.astype(jnp.float32) * wide[:, begin : begin + CHUNK]
            for lane in range(0, CHUNK, 128):
                piece = scaled[:, lane : lane + 128]
                means = piece if means is None else means + piece
            product = jnp.dot(
                values, factor_ref[begin : begin + CHUNK, :], preferred_element_type=jnp.float32
            )
            total = product if total is None else total + product
        part[step] = total
        begin = 0
        for at, size in zip(where, sizes):
            mean_acc[pl.ds(at, size), :] = means[begin : begin + size, :]
            begin += size

    def send(source, target, ssem, rsem, device):
        return pltpu.make_async_remote_copy(
            src_ref=source, dst_ref=target, send_sem=ssem, recv_sem=rsem, device_id={"trn": device}
        )

    def copy_y(s):
        return send(part.at[s, 4 * gb : 4 * gb + 2 * ga], got_y.at[s], s_y.at[s], r_y.at[s], other)

    def first_b(s, got, begin, ssem, rsem, device):
        return send(part.at[s, begin : begin + 2 * gb], got.at[s], ssem.at[s], rsem.at[s], device)

    def first_a(s, got, begin, ssem, rsem, device):
        return send(part.at[s, begin : begin + ga], got.at[s], ssem.at[s], rsem.at[s], device)

    def onward(s, got, ssem, rsem, device):
        return send(got.at[s], got.at[s], ssem.at[s], rsem.at[s], device)

    def swap(s, got):
        theirs = pl.ds(pl.multiple_of((1 - y) * gb, 8), gb)
        return send(got.at[s, theirs], got_x.at[s], s_x.at[s], r_x.at[s], other)

    def square(values):
        total = None
        for lane in range(0, values.shape[1], 128):
            piece = values[:, lane : lane + 128]
            total = piece * piece if total is None else total + piece * piece
        return total

    chains_b = (
        (got_br, 0, s_br, r_br, z, up, LAG_B),
        (got_bl, 2 * gb, s_bl, r_bl, last - z, down, LAG_B),
    )
    chains_a = (
        (got_ar, 4 * gb + 3 * ga, s_ar, r_ar, z, up, LAG_A),
        (got_al, 4 * gb + 2 * ga, s_al, r_al, last - z, down, LAG_A),
    )

    def lag_of(hop, table):
        value = table[1]
        for index in range(2, LINE):
            value = jnp.where(hop == index, table[index], value)
        return value

    def inside(s):
        return (s >= 0) & (s < STEPS)

    fetch.wait()
    compute(0)
    between = (z > 0) & (z < last)
    pl.when(between)(lambda: pl.semaphore_wait(barrier, 3))
    pl.when(jnp.logical_not(between))(lambda: pl.semaphore_wait(barrier, 2))


    def turn(it, carry):
        @pl.when((it > 0) & (it < STEPS))
        def _():
            compute(it)

        @pl.when(it < STEPS)
        def _():
            copy_y(it).start()
            for got, begin, ssem, rsem, hop, device, _ in chains_b:
                @pl.when(hop == 0)
                def _():
                    first_b(it, got, begin, ssem, rsem, device).start()

        for got, begin, ssem, rsem, hop, device, lags in chains_b:
            s = it - lag_of(hop, lags)

            @pl.when((hop > 0) & inside(s))
            def _():
                onward(s, got, ssem, rsem, device).wait_recv()
                got[s] = got[s] + part[s, begin : begin + 2 * gb]

                @pl.when(hop < last)
                def _():
                    onward(s, got, ssem, rsem, device).start()

                @pl.when(hop == last)
                def _():
                    swap(s, got).start()

        s_here = it - LAG_Y

        @pl.when(inside(s_here))
        def _():
            copy_y(s_here).wait_recv()
            kept = slice(4 * gb + 2 * ga, 4 * gb + 4 * ga)
            part[s_here, kept] = part[s_here, kept] + got_y[s_here]
            for got, begin, ssem, rsem, hop, device, _ in chains_a:
                @pl.when(hop == 0)
                def _():
                    first_a(s_here, got, begin, ssem, rsem, device).start()

        for got, begin, ssem, rsem, hop, device, lags in chains_a:
            s = it - lag_of(hop, lags)

            @pl.when((hop > 0) & inside(s))
            def _():
                onward(s, got, ssem, rsem, device).wait_recv()

                @pl.when(hop < last)
                def _():
                    got[s] = got[s] + part[s, begin : begin + ga]
                    onward(s, got, ssem, rsem, device).start()

                @pl.when(hop == last)
                def _():
                    at = pl.multiple_of(gb * STEPS + s * ga, 8)
                    var_acc[pl.ds(at, ga), :] = square(got[s] + part[s, begin : begin + ga])

        s_last = it - LAG_X
        for got, hop in ((got_br, z), (got_bl, last - z)):
            @pl.when((hop == last) & inside(s_last))
            def _():
                swap(s_last, got).wait_recv()
                mine = pl.ds(pl.multiple_of(y * gb, 8), gb)
                at = pl.multiple_of(s_last * gb, 8)
                var_acc[pl.ds(at, gb), :] = square(got[s_last, mine] + got_x[s_last])

        @pl.when(it == STEPS + LAG_Y)
        def _():
            for index in range(rows // 128):
                block = mean_acc[index * 128 : (index + 1) * 128, :]
                mean_box[me, index : index + 1, :] = jnp.sum(block.T, axis=0, keepdims=True)

            def tell(k, carry):
                mean_copy(k).start()
                return carry

            lax.fori_loop(1, count, tell, 0)

        return carry

    def mean_copy(k):
        return send(
            mean_box.at[me], mean_box.at[me], s_mean.at[k], r_mean.at[k], lax.rem(me + k, count)
        )

    lax.fori_loop(0, STEPS + max(LAG_X, LAG_A[-1]), turn, 0)

    owner = jnp.where(z == last, 2, 0) + y
    ends = (z == 0) | (z == last)

    def var_copy(k, who):
        return send(var_box.at[who], var_box.at[who], s_var.at[k], r_var.at[who], lax.rem(me + k, count))

    @pl.when(ends)
    def _():
        for index in range(span // 128):
            block = var_acc[index * 128 : (index + 1) * 128, :]
            var_box[owner, index : index + 1, :] = 1.0 - jnp.sum(block.T, axis=0, keepdims=True)

        def tell(k, carry):
            var_copy(k, owner).start()
            return carry

        lax.fori_loop(1, count, tell, 0)

    def hear(k, carry):
        mean_copy(k).wait()
        return carry

    lax.fori_loop(1, count, hear, 0)
    total = mean_box[0]
    for index in range(1, count):
        total = total + mean_box[index]
    out_ref[: rows // 128, :] = total

    def settle(s, carry):
        copy_y(s).wait_send()
        for got, begin, ssem, rsem, hop, device, _ in chains_b:
            @pl.when(hop == 0)
            def _():
                first_b(s, got, begin, ssem, rsem, device).wait_send()

            @pl.when((hop > 0) & (hop < last))
            def _():
                onward(s, got, ssem, rsem, device).wait_send()

            @pl.when(hop == last)
            def _():
                swap(s, got).wait_send()

        for got, begin, ssem, rsem, hop, device, _ in chains_a:
            @pl.when(hop == 0)
            def _():
                first_a(s, got, begin, ssem, rsem, device).wait_send()

            @pl.when((hop > 0) & (hop < last))
            def _():
                onward(s, got, ssem, rsem, device).wait_send()

        return carry

    lax.fori_loop(0, STEPS, settle, 0)

    for who in range(4):
        @pl.when(jnp.logical_not(ends) | (owner != who))
        def _():
            var_copy(1, who).wait_recv()

    lines = span // 128
    for who in range(4):
        begin = rows // 128 + who * lines
        out_ref[begin : begin + lines, :] = var_box[who]

    @pl.when(ends)
    def _():
        def done(k, carry):
            var_copy(k, owner).wait_send()
            return carry

        lax.fori_loop(1, count, done, 0)


def fused(test_points, train_points, weights, factor, *, count):
    dim, rows = test_points.shape
    local = train_points.shape[1]
    width = factor.shape[1]
    depth = -(-(dim + 16) // 128) * 128
    quarter = rows // (4 * STEPS)
    gb = quarter * SHARE // 8
    ga = quarter - gb
    dma = pltpu.SemaphoreType.DMA
    f32 = jnp.float32
    sems = [dma((STEPS,))] * 12 + [dma((count,)), dma((count,)), dma((count,)), dma((4,))]
    out = pl.pallas_call(
        kernel,
        out_shape=jax.ShapeDtypeStruct((rows // 64, 128), f32),
        in_specs=[pl.BlockSpec(memory_space=pltpu.VMEM)] * 3
        + [pl.BlockSpec(memory_space=pl.ANY)],
        out_specs=pl.BlockSpec(memory_space=pltpu.VMEM),
        scratch_shapes=[
            pltpu.VMEM((rows, depth), f32),
            pltpu.VMEM((depth, local), jnp.bfloat16),
            pltpu.VMEM((1, local), f32),
            pltpu.VMEM((STEPS, 4 * quarter, width), f32),
            pltpu.VMEM((STEPS, 2 * ga, width), f32),
            pltpu.VMEM((STEPS, 2 * gb, width), f32),
            pltpu.VMEM((STEPS, 2 * gb, width), f32),
            pltpu.VMEM((STEPS, ga, width), f32),
            pltpu.VMEM((STEPS, ga, width), f32),
            pltpu.VMEM((STEPS, gb, width), f32),
            pltpu.VMEM((rows, 128), f32),
            pltpu.VMEM((rows // 4, 128), f32),
            pltpu.VMEM((count, rows // 128, 128), f32),
            pltpu.VMEM((4, rows // 512, 128), f32),
        ] + sems + [pltpu.VMEM((local, width), jnp.bfloat16), dma],
        compiler_params=pltpu.CompilerParams(
            collective_id=0, has_side_effects=True, vmem_limit_bytes=56 * 1024 * 1024
        ),
    )(test_points, train_points, weights.reshape(1, local), factor)
    lines = rows // 128
    return out[:lines].reshape(rows), out[lines:].reshape(rows)


def on_device(test_points, train_points, weights, factor):
    rows = test_points.shape[1]
    local = train_points.shape[1]
    dim = test_points.shape[0]
    width = factor.shape[1]
    test_sq = jnp.sum(test_points.astype(jnp.float32) ** 2, axis=0)
    block = math.gcd(local, 1024)
    turns = local // block

    def step(index, carry):
        mean_acc, proj_acc = carry
        start = (index * block).astype(jnp.int32)
        points = lax.dynamic_slice_in_dim(train_points, start, block, 1)
        wblock = lax.dynamic_slice_in_dim(weights, start, block, 0)
        fblock = lax.dynamic_slice_in_dim(factor, start, block, 0)
        train_sq = jnp.sum(points.astype(jnp.float32) ** 2, axis=0)
        cross = lax.dot_general(
            test_points, points, (((0,), (0,)), ((), ())), preferred_element_type=jnp.float32
        )
        kernel = jnp.exp(
            -(test_sq[:, None] + train_sq[None, :] - 2.0 * cross) * (4.0 / dim)
        ).astype(jnp.bfloat16)
        mean_acc = mean_acc + jnp.dot(kernel, wblock, preferred_element_type=jnp.float32)
        proj_acc = proj_acc + jnp.dot(kernel, fblock, preferred_element_type=jnp.float32)
        return (mean_acc, proj_acc)

    init = (jnp.zeros((rows,), jnp.float32), jnp.zeros((rows, width), jnp.float32))
    mean_part, proj_part = lax.fori_loop(0, turns, step, init)
    mean_share, proj_share = (
        lax.psum_scatter(mean_part, "trn", scatter_dimension=0, tiled=True),
        lax.psum_scatter(proj_part, "trn", scatter_dimension=0, tiled=True),
    )
    var_share = 1.0 - jnp.sum(proj_share * proj_share, axis=1)
    mean, variance = (
        lax.all_gather(mean_share, "trn", axis=0, tiled=True),
        lax.all_gather(var_share, "trn", axis=0, tiled=True),
    )
    return (mean, variance)


def solution(mesh):
    in_specs = (
        P(None, ("grp", "tst")),
        P(None, ("grp", "trn")),
        P(("grp", "trn")),
        P(("grp", "trn"), None),
    )
    out_specs = (P(("grp", "tst")), P(("grp", "tst")))
    count = mesh.shape["trn"]
    body = functools.partial(fused, count=count) if count == 2 * LINE else on_device
    return jax.shard_map(
        body, mesh=mesh, in_specs=in_specs, out_specs=out_specs, check_vma=False
    )
```

profile of v0, /device:TPU:0, one launch (start us, length us, event | category | flops | bytes accessed | tf_op | source)
XLA Modules:
  0.0 63.3 jit_solution(1846042984515975034)
XLA Ops:
  0.6 1.3 %reshape.13.weights_ref = bf16[1,4096]{1,0:T(2,128)(2,1)} reshape(bf16[4096]{0:T(1024)(128)(2,1)} %param.6) | data formatting | bytes 16384 | tf_op jit(solution)/shard_map/reshape | solution.py:394
  1.9 60.0 %shard_map.59 = f32[32,128]{1,0:T(8,128)} custom-call(bf16[64,2048]{1,0:T(8,128)(2,1)} %test_ref.1, bf16[64,4096]{1,0:T(8,128)(2,1)} %train_ref.1, bf16[1,4096]{1,0:T(2,128)(2,1)} %reshape.13.weights_ref, bf16[4096,512]{1,0:T(8,128)(2,1)} %factor_hbm.1), custom_call_target="tpu_custom_call" | custom-call | tf_op jit(solution)/shard_map/pallas_call | solution.py:369
  62.0 1.3 %slice_bitcast_fusion = (f32[2048]{0:T(1024)}, f32[2048]{0:T(1024)}) fusion(f32[32,128]{1,0:T(8,128)} %shard_map.59), kind=kLoop, calls=%fused_computation | loop fusion | bytes 32768 | tf_op jit(solution)/shard_map/reshape | solution.py:396
where the time goes:
time: 63.5 us; the launch traced here: 63.3 us
  Pallas kernels  60 us (94%)
  local copies, waits for them, and re-layouts  2.63 us (4%)
  between operations  0.64 us (1%)
    pallas_call x1, Pallas kernels, fused(): pl.pallas_call(kernel, out_shape=jax.ShapeDtypeStruct((rows // 64, 128),...  60 us
    reshape x1, local copies, waits for them, and re-layouts, fused(): return (out[:lines].reshape(rows), out[lines:].reshape(rows))  1.32 us
    reshape x1, local copies, waits for them, and re-layouts, fused(): weights.reshape(1, local)  1.31 us

commit v1 on v0

v1 whole, which is shorter than its diff:
```python
import functools
import math

import jax
import jax.numpy as jnp
from jax import lax
from jax.experimental import pallas as pl
from jax.experimental.pallas import tpu as pltpu
from jax.sharding import PartitionSpec as P

LOG2E = 1.4426950408889634
BLOCK = 128
CHUNK = 1024
LINE = 4
KINDS = ((8, 16, 16), (8, 8, 24))
LAG_Y = 3
LAG_B = (0, 2, 4, 11)
LAG_A = (3, 5, 8, 25)
LAG_SWAP = 13
LAG_X = 23
MEAN_AT = 1
MEAN_ON = 4


def pieces(value):
    high = value.astype(jnp.bfloat16).astype(jnp.float32)
    rest = value - high
    middle = rest.astype(jnp.bfloat16).astype(jnp.float32)
    low = (rest - middle).astype(jnp.bfloat16).astype(jnp.float32)
    return high, middle, low


def pick(row, table, default):
    value = default
    for index, entry in table:
        value = jnp.where(row == index, entry, value)
    return value


def kinds_of(rows):
    unit = rows // BLOCK // sum(count for count, _, _ in KINDS)
    table, begin, base = [], 0, 0
    for count, gb, ga in KINDS:
        count = count * unit
        table.append((begin, count, gb, ga, base))
        begin += count
        base += count * (gb + ga)
    return tuple(table)


def kernel(
    test_hbm, train_hbm, weights_hbm, factor_hbm, out_ref,
    test_ref, train_ref, weights_ref, factor_ref, in_sems,
    test_aug, train_aug, wide, left_ref, part, mean_acc, var_acc, mean_box, var_box,
    s_y, r_y, s_br, r_br, s_bl, r_bl, s_ar, r_ar, s_al, r_al, s_x, r_x,
    s_mean, r_mean, s_var, r_var, *got,
):
    count = var_box.shape[0] * 2
    pair = count // LINE
    last = LINE - 1
    me = lax.axis_index("trn")
    z = me // pair
    y = me % pair
    dim, rows = test_ref.shape
    local = train_ref.shape[1]
    depth = test_aug.shape[1]
    steps = rows // BLOCK
    kinds = kinds_of(rows)
    span = rows // 4
    other = z * pair + (1 - y)
    up, down = me + pair, me - pair
    chunks = local // CHUNK

    barrier = pltpu.get_barrier_semaphore()
    for k in range(1, count):
        pl.semaphore_signal(barrier, inc=1, device_id={"trn": lax.rem(me + k, count)})

    def fetch(index, source, target):
        return pltpu.make_async_copy(source, target, in_sems.at[index])

    fetch_train = fetch(0, train_hbm, train_ref)
    fetch_test = fetch(1, test_hbm, test_ref)
    fetch_weights = fetch(2, weights_hbm, weights_ref)

    def fetch_factor(index):
        block = pl.ds(index * CHUNK, CHUNK)
        return fetch(3 + index, factor_hbm.at[block], factor_ref.at[block])

    fetch_train.start()
    fetch_test.start()
    fetch_weights.start()
    for index in range(chunks):
        fetch_factor(index).start()

    fetch_train.wait()

    def prepare_train(index, carry):
        cols = pl.ds(pl.multiple_of(index * 512, 512), 512)
        points = train_ref[:, cols]
        squares = points.astype(jnp.float32) ** 2
        norm = jnp.sum(squares, axis=0, keepdims=True) * (-4.0 / dim)
        high, middle, low = pieces(norm)
        row = lax.broadcasted_iota(jnp.int32, (16, 512), 0)
        one = jnp.float32(1.0)
        extra = pick(row, ((0, one), (1, one), (2, one), (3, high), (4, middle), (5, low)), jnp.float32(0.0))
        train_aug[:dim, cols] = points
        train_aug[dim : dim + 16, cols] = extra.astype(jnp.bfloat16)
        train_aug[dim + 16 :, cols] = jnp.zeros((depth - dim - 16, 512), jnp.bfloat16)
        return carry

    lax.fori_loop(0, local // 512, prepare_train, 0)
    fetch_test.wait()

    def prepare_test(index, carry):
        cols = pl.ds(pl.multiple_of(index * 256, 256), 256)
        points = test_ref[:, cols].astype(jnp.float32)
        norm = jnp.sum(points * points, axis=0, keepdims=True) * (-4.0 / dim)
        high, middle, low = pieces(norm)
        row = lax.broadcasted_iota(jnp.int32, (8, 256), 0)
        one = jnp.float32(1.0)
        extra = pick(row, ((0, high), (1, middle), (2, low), (3, one), (4, one), (5, one)), jnp.float32(0.0))
        whole = jnp.concatenate(
            [points * (8.0 / dim), extra, jnp.zeros((depth - dim - 8, 256), jnp.float32)], axis=0
        )
        test_aug[cols, :] = whole.T
        return carry

    lax.fori_loop(0, rows // 256, prepare_test, 0)
    fetch_weights.wait()
    for index in range(local // 128):
        wide[:, index * 128 : (index + 1) * 128] = weights_ref[index : index + 1, :].astype(jnp.float32)

    def places(kind, step):
        begin, number, gb, ga, base = kind
        index = step - begin

        def row_of(owner, early):
            inner = base + (number * gb + index * ga if early else index * gb)
            return pl.multiple_of(owner * span + inner, 8)

        where = (
            row_of(2, False), row_of(3, False), row_of(0, False), row_of(1, False),
            row_of(1 - y, True), row_of(3 - y, True), row_of(y, True), row_of(2 + y, True),
        )
        return tuple(zip(where, (gb,) * 4 + (ga,) * 4))

    def compute(step, first=False):
        for kind in kinds:
            if first and kind[0] > 0:
                continue

            def gather():
                left_ref[...] = jnp.concatenate(
                    [test_aug[pl.ds(at, size), :] for at, size in places(kind, step)], axis=0
                ).astype(jnp.bfloat16)

            if first:
                gather()
            else:
                pl.when((step >= kind[0]) & (step < kind[0] + kind[1]))(gather)
        left = left_ref[...]
        total = None
        means = None
        for index in range(chunks):
            begin = index * CHUNK
            power = jnp.dot(
                left, train_aug[:, begin : begin + CHUNK], preferred_element_type=jnp.float32
            )
            values = jnp.exp2(power * LOG2E).astype(jnp.bfloat16)
            scaled = values.astype(jnp.float32) * wide[:, begin : begin + CHUNK]
            for lane in range(0, CHUNK, 128):
                piece = scaled[:, lane : lane + 128]
                means = piece if means is None else means + piece
            if first:
                fetch_factor(index).wait()
            product = jnp.dot(
                values, factor_ref[begin : begin + CHUNK, :], preferred_element_type=jnp.float32
            )
            total = product if total is None else total + product
        part[step] = total
        mean_acc[pl.ds(pl.multiple_of(step * BLOCK, BLOCK), BLOCK), :] = means

    def send(source, target, ssem, rsem, device):
        return pltpu.make_async_remote_copy(
            src_ref=source, dst_ref=target, send_sem=ssem, recv_sem=rsem, device_id={"trn": device}
        )

    def square(values):
        total = None
        for lane in range(0, values.shape[1], 128):
            piece = values[:, lane : lane + 128]
            total = piece * piece if total is None else total + piece * piece
        return total

    class Kind:
        def __init__(self, kind, buffers):
            self.begin, self.number, self.gb, self.ga, self.base = kind
            self.got_y, self.got_br, self.got_bl, self.got_ar, self.got_al, self.got_x = buffers
            gb, ga = self.gb, self.ga
            self.chains_b = (
                (self.got_br, 0, s_br, r_br, z, up),
                (self.got_bl, 2 * gb, s_bl, r_bl, last - z, down),
            )
            self.chains_a = (
                (self.got_ar, 4 * gb + 3 * ga, s_ar, r_ar, z, up),
                (self.got_al, 4 * gb + 2 * ga, s_al, r_al, last - z, down),
            )

        def has(self, s):
            return (s >= self.begin) & (s < self.begin + self.number)

        def copy_y(self, s):
            gb, ga = self.gb, self.ga
            source = part.at[s, 4 * gb : 4 * gb + 2 * ga]
            return send(source, self.got_y.at[s - self.begin], s_y.at[s], r_y.at[s], other)

        def first_b(self, s, chain):
            got, begin, ssem, rsem, _, device = chain
            source = part.at[s, begin : begin + 2 * self.gb]
            return send(source, got.at[s - self.begin], ssem.at[s], rsem.at[s], device)

        def first_a(self, s, chain):
            got, begin, ssem, rsem, _, device = chain
            source = part.at[s, begin : begin + self.ga]
            return send(source, got.at[s - self.begin], ssem.at[s], rsem.at[s], device)

        def onward(self, s, chain):
            got, _, ssem, rsem, _, device = chain
            j = s - self.begin
            return send(got.at[j], got.at[j], ssem.at[s], rsem.at[s], device)

        def swap(self, s, got):
            j = s - self.begin
            theirs = pl.ds(pl.multiple_of((1 - y) * self.gb, 8), self.gb)
            return send(got.at[j, theirs], self.got_x.at[j], s_x.at[s], r_x.at[s], other)

    table = [Kind(kind, got[6 * i : 6 * i + 6]) for i, kind in enumerate(kinds)]

    def lag_of(hop, lags):
        value = lags[1]
        for index in range(2, LINE):
            value = jnp.where(hop == index, lags[index], value)
        return value

    def mean_swap():
        return send(mean_box.at[z], mean_box.at[LINE], s_mean.at[0], r_mean.at[0], other)

    def mean_copy(k):
        target = lax.rem(me + k * pair, count)
        return send(mean_box.at[z], mean_box.at[z], s_mean.at[k], r_mean.at[k], target)

    compute(0, True)
    pl.semaphore_wait(barrier, count - 1)

    def turn(it, carry):
        @pl.when((it > 0) & (it < steps))
        def _():
            compute(it)

        for kind in table:
            @pl.when(kind.has(it))
            def _():
                for chain in kind.chains_b:
                    @pl.when(chain[4] == 0)
                    def _():
                        kind.first_b(it, chain).start()
                kind.copy_y(it).start()

        for kind in table:
            gb = kind.gb
            for chain in kind.chains_b:
                got, begin, hop = chain[0], chain[1], chain[4]
                s = it - lag_of(hop, LAG_B)

                @pl.when((hop > 0) & kind.has(s))
                def _():
                    kind.onward(s, chain).wait_recv()
                    j = s - kind.begin
                    got[j] = got[j] + part[s, begin : begin + 2 * gb]

                    @pl.when(hop < last)
                    def _():
                        kind.onward(s, chain).start()

        for kind in table:
            gb, ga = kind.gb, kind.ga
            s_here = it - LAG_Y

            @pl.when(kind.has(s_here))
            def _():
                kind.copy_y(s_here).wait_recv()
                kept = slice(4 * gb + 2 * ga, 4 * gb + 4 * ga)
                part[s_here, kept] = part[s_here, kept] + kind.got_y[s_here - kind.begin]

            s_go = it - LAG_A[0]

            @pl.when(kind.has(s_go))
            def _():
                for chain in kind.chains_a:
                    @pl.when(chain[4] == 0)
                    def _():
                        kind.first_a(s_go, chain).start()

        for kind in table:
            gb, ga = kind.gb, kind.ga
            for chain in kind.chains_a:
                got, begin, hop = chain[0], chain[1], chain[4]
                s = it - lag_of(hop, LAG_A)

                @pl.when((hop > 0) & kind.has(s))
                def _():
                    kind.onward(s, chain).wait_recv()
                    j = s - kind.begin

                    @pl.when(hop < last)
                    def _():
                        got[j] = got[j] + part[s, begin : begin + ga]
                        kind.onward(s, chain).start()

                    @pl.when(hop == last)
                    def _():
                        at = pl.multiple_of(kind.base + gb * kind.number + j * ga, 8)
                        var_acc[pl.ds(at, ga), :] = square(got[j] + part[s, begin : begin + ga])

        for kind in table:
            gb = kind.gb
            s_swap = it - LAG_SWAP
            s_last = it - LAG_X
            for got, hop in ((kind.got_br, z), (kind.got_bl, last - z)):
                @pl.when((hop == last) & kind.has(s_swap))
                def _():
                    kind.swap(s_swap, got).start()

                @pl.when((hop == last) & kind.has(s_last))
                def _():
                    kind.swap(s_last, got).wait_recv()
                    j = s_last - kind.begin
                    mine = pl.ds(pl.multiple_of(y * gb, 8), gb)
                    at = pl.multiple_of(kind.base + j * gb, 8)
                    var_acc[pl.ds(at, gb), :] = square(got[j, mine] + kind.got_x[j])

        @pl.when(it == steps + MEAN_AT)
        def _():
            for kind in kinds:
                def place(step, carry):
                    begin = pl.multiple_of(step * BLOCK, BLOCK)
                    for at, size in places(kind, step):
                        test_aug[pl.ds(at, size), :] = mean_acc[pl.ds(begin, size), :]
                        begin = pl.multiple_of(begin + size, 8)
                    return carry

                lax.fori_loop(kind[0], kind[0] + kind[1], place, 0)
            for index in range(rows // 128):
                block = test_aug[index * 128 : (index + 1) * 128, :]
                mean_box[z, index : index + 1, :] = jnp.sum(block.T, axis=0, keepdims=True)
            mean_swap().start()

        @pl.when(it == steps + MEAN_ON)
        def _():
            mean_swap().wait()
            mean_box[z] = mean_box[z] + mean_box[LINE]
            for k in range(1, LINE):
                mean_copy(k).start()

        return carry

    lax.fori_loop(0, steps + max(LAG_X, LAG_A[-1]), turn, 0)

    owner = jnp.where(z == last, 2, 0) + y
    ends = (z == 0) | (z == last)

    def var_copy(k, who):
        return send(var_box.at[who], var_box.at[who], s_var.at[k], r_var.at[who], lax.rem(me + k, count))

    @pl.when(ends)
    def _():
        for index in range(span // 128):
            block = var_acc[index * 128 : (index + 1) * 128, :]
            var_box[owner, index : index + 1, :] = 1.0 - jnp.sum(block.T, axis=0, keepdims=True)
        for k in range(1, count):
            var_copy(k, owner).start()

    for k in range(1, LINE):
        mean_copy(k).wait()
    total = mean_box[0]
    for index in range(1, LINE):
        total = total + mean_box[index]
    out_ref[: rows // 128, :] = total

    for kind in table:
        def settle(s, carry):
            kind.copy_y(s).wait_send()
            for chain in kind.chains_b:
                got, hop = chain[0], chain[4]

                @pl.when(hop == 0)
                def _():
                    kind.first_b(s, chain).wait_send()

                @pl.when((hop > 0) & (hop < last))
                def _():
                    kind.onward(s, chain).wait_send()

                @pl.when(hop == last)
                def _():
                    kind.swap(s, got).wait_send()

            for chain in kind.chains_a:
                hop = chain[4]

                @pl.when(hop == 0)
                def _():
                    kind.first_a(s, chain).wait_send()

                @pl.when((hop > 0) & (hop < last))
                def _():
                    kind.onward(s, chain).wait_send()

            return carry

        lax.fori_loop(kind.begin, kind.begin + kind.number, settle, 0)

    for who in range(4):
        @pl.when(jnp.logical_not(ends) | (owner != who))
        def _():
            var_copy(1, who).wait_recv()

    lines = span // 128
    for who in range(4):
        begin = rows // 128 + who * lines
        out_ref[begin : begin + lines, :] = var_box[who]

    @pl.when(ends)
    def _():
        for k in range(1, count):
            var_copy(k, owner).wait_send()


def fused(test_points, train_points, weights, factor, *, count):
    dim, rows = test_points.shape
    local = train_points.shape[1]
    width = factor.shape[1]
    depth = -(-(dim + 16) // 128) * 128
    steps = rows // BLOCK
    dma = pltpu.SemaphoreType.DMA
    f32 = jnp.float32
    sems = [dma((steps,))] * 12 + [dma((LINE,)), dma((LINE,)), dma((count,)), dma((4,))]
    boxes = []
    for _, number, gb, ga, _ in kinds_of(rows):
        for size in (2 * ga, 2 * gb, 2 * gb, ga, ga, gb):
            boxes.append(pltpu.VMEM((number, size, width), f32))
    out = pl.pallas_call(
        kernel,
        out_shape=jax.ShapeDtypeStruct((rows // 64, 128), f32),
        in_specs=[pl.BlockSpec(memory_space=pl.ANY)] * 4,
        out_specs=pl.BlockSpec(memory_space=pltpu.VMEM),
        scratch_shapes=[
            pltpu.VMEM((dim, rows), jnp.bfloat16),
            pltpu.VMEM((dim, local), jnp.bfloat16),
            pltpu.VMEM((local // 128, 128), jnp.bfloat16),
            pltpu.VMEM((local, width), jnp.bfloat16),
            dma((3 + local // CHUNK,)),
            pltpu.VMEM((rows, depth), f32),
            pltpu.VMEM((depth, local), jnp.bfloat16),
            pltpu.VMEM((1, local), f32),
            pltpu.VMEM((BLOCK, depth), jnp.bfloat16),
            pltpu.VMEM((steps, BLOCK, width), f32),
            pltpu.VMEM((rows, 128), f32),
            pltpu.VMEM((rows // 4, 128), f32),
            pltpu.VMEM((LINE + 1, rows // 128, 128), f32),
            pltpu.VMEM((4, rows // 512, 128), f32),
        ] + sems + boxes,
        compiler_params=pltpu.CompilerParams(
            collective_id=0, has_side_effects=True, vmem_limit_bytes=56 * 1024 * 1024
        ),
    )(test_points, train_points, weights.reshape(local // 128, 128), factor)
    lines = rows // 128
    return out[:lines].reshape(rows), out[lines:].reshape(rows)


def on_device(test_points, train_points, weights, factor):
    rows = test_points.shape[1]
    local = train_points.shape[1]
    dim = test_points.shape[0]
    width = factor.shape[1]
    test_sq = jnp.sum(test_points.astype(jnp.float32) ** 2, axis=0)
    block = math.gcd(local, 1024)
    turns = local // block

    def step(index, carry):
        mean_acc, proj_acc = carry
        start = (index * block).astype(jnp.int32)
        points = lax.dynamic_slice_in_dim(train_points, start, block, 1)
        wblock = lax.dynamic_slice_in_dim(weights, start, block, 0)
        fblock = lax.dynamic_slice_in_dim(factor, start, block, 0)
        train_sq = jnp.sum(points.astype(jnp.float32) ** 2, axis=0)
        cross = lax.dot_general(
            test_points, points, (((0,), (0,)), ((), ())), preferred_element_type=jnp.float32
        )
        kernel = jnp.exp(
            -(test_sq[:, None] + train_sq[None, :] - 2.0 * cross) * (4.0 / dim)
        ).astype(jnp.bfloat16)
        mean_acc = mean_acc + jnp.dot(kernel, wblock, preferred_element_type=jnp.float32)
        proj_acc = proj_acc + jnp.dot(kernel, fblock, preferred_element_type=jnp.float32)
        return (mean_acc, proj_acc)

    init = (jnp.zeros((rows,), jnp.float32), jnp.zeros((rows, width), jnp.float32))
    mean_part, proj_part = lax.fori_loop(0, turns, step, init)
    mean_share, proj_share = (
        lax.psum_scatter(mean_part, "trn", scatter_dimension=0, tiled=True),
        lax.psum_scatter(proj_part, "trn", scatter_dimension=0, tiled=True),
    )
    var_share = 1.0 - jnp.sum(proj_share * proj_share, axis=1)
    mean, variance = (
        lax.all_gather(mean_share, "trn", axis=0, tiled=True),
        lax.all_gather(var_share, "trn", axis=0, tiled=True),
    )
    return (mean, variance)


def solution(mesh):
    in_specs = (
        P(None, ("grp", "tst")),
        P(None, ("grp", "trn")),
        P(("grp", "trn")),
        P(("grp", "trn"), None),
    )
    out_specs = (P(("grp", "tst")), P(("grp", "tst")))
    count = mesh.shape["trn"]
    body = functools.partial(fused, count=count) if count == 2 * LINE else on_device
    return jax.shard_map(
        body, mesh=mesh, in_specs=in_specs, out_specs=out_specs, check_vma=False
    )
```

time: 63.5 us -> 58.5 us (0.921)
  Pallas kernels: 60 us -> 56.3 us
  local copies, waits for them, and re-layouts: 2.63 us -> 1.32 us
    pallas_call x1, Pallas kernels: 60 us -> 56.3 us  [fused(): pl.pallas_call(kernel, out_shape=jax.ShapeDtypeStruct((rows // 64, 128),...]
    reshape x1 -> x0, local copies, waits for them, and re-layouts: 1.31 us -> none  [fused(): weights.reshape(1, local)]
where the time goes in v1:
time: 58.5 us; the launch traced here: 58.3 us
  Pallas kernels  56.3 us (96%)
  local copies, waits for them, and re-layouts  1.32 us (2%)
  between operations  0.64 us (1%)
    pallas_call x1, Pallas kernels, fused(): pl.pallas_call(kernel, out_shape=jax.ShapeDtypeStruct((rows // 64, 128),...  56.3 us
    reshape x1, local copies, waits for them, and re-layouts, fused(): return (out[:lines].reshape(rows), out[lines:].reshape(rows))  1.32 us

profile of v1, /device:TPU:0, one launch (start us, length us, event | category | flops | bytes accessed | tf_op | source)
XLA Modules:
  0.0 58.3 jit_solution(1702049343787110992)
XLA Ops:
  0.6 56.3 %shard_map.59 = f32[32,128]{1,0:T(8,128)} custom-call(bf16[64,2048]{1,0:T(8,128)(2,1)} %test_hbm.1, bf16[64,4096]{1,0:T(8,128)(2,1)} %train_hbm.1, bf16[32,128]{1,0:T(8,128)(2,1)} %bitcast.5, bf16[4096,512]{1,0:T(8,128)(2,1)} %factor_hbm.1), custom_call_target="tpu_custom_call" | custom-call | tf_op jit(solution)/shard_map/pallas_call | solution.py:452
  57.0 1.3 %slice_bitcast_fusion = (f32[2048]{0:T(1024)}, f32[2048]{0:T(1024)}) fusion(f32[32,128]{1,0:T(8,128)} %shard_map.59), kind=kLoop, calls=%fused_computation | loop fusion | bytes 32768 | tf_op jit(solution)/shard_map/reshape | solution.py:478

commit v2 on v1

v2 whole, which is shorter than its diff:
```python
import functools
import math

import jax
import jax.numpy as jnp
from jax import lax
from jax.experimental import pallas as pl
from jax.experimental.pallas import tpu as pltpu
from jax.sharding import PartitionSpec as P

LOG2E = 1.4426950408889634
BLOCK = 128
CHUNK = 1024
LINE = 4
KINDS = ((10, 16, 16), (4, 8, 24))
MIDDLE = 2
LAG_Y = 3
LAG_B = (0, 2, 4, 11)
LAG_A = (3, 5, 8, 18)
LAG_SWAP = 11
LAG_X = 18
LAG_M = (4, 6, 17)
MEAN_AT = 1
MEAN_ON = 4


def pieces(value):
    high = value.astype(jnp.bfloat16).astype(jnp.float32)
    rest = value - high
    middle = rest.astype(jnp.bfloat16).astype(jnp.float32)
    low = (rest - middle).astype(jnp.bfloat16).astype(jnp.float32)
    return high, middle, low


def pick(row, table, default):
    value = default
    for index, entry in table:
        value = jnp.where(row == index, entry, value)
    return value


def kinds_of(rows):
    unit = rows // BLOCK // (MIDDLE + sum(count for count, _, _ in KINDS))
    table, begin, base = [], 0, 0
    for count, gb, ga in KINDS:
        count = count * unit
        table.append((begin, count, gb, ga, base))
        begin += count
        base += count * (gb + ga)
    return tuple(table), (begin, MIDDLE * unit, BLOCK // 4, base)


def kernel(
    test_hbm, train_hbm, weights_hbm, factor_hbm, out_ref,
    test_ref, train_ref, weights_ref, factor_ref, in_sems,
    test_aug, train_aug, wide, left_ref, part, mean_acc, var_acc, mean_box, var_box, mid_box,
    s_y, r_y, s_b, rp_b, sq_b, rq_b, s_a, rp_a, sq_a, rq_a, s_x, r_x,
    s_yn, r_yn, s_mf, r_mf, s_mn, r_mn, s_mx, r_mx,
    s_mean, r_mean, s_var, r_var, r_mid, got_yf, got_yn, got_mf, got_mn, got_mx, *got, count,
):
    pair = count // LINE
    last = LINE - 1
    me = lax.axis_index("trn")
    z = me // pair
    y = me % pair
    dim, rows = test_ref.shape
    local = train_ref.shape[1]
    depth = test_aug.shape[1]
    steps = rows // BLOCK
    kinds, middle = kinds_of(rows)
    span = rows // 4
    other = z * pair + (1 - y)
    low = z < 2
    toward = jnp.where(low, me + pair, me - pair)
    back = jnp.where(low, me - pair, me + pair)
    far = jnp.where(low, 2, 0)
    near = 2 - far
    owner = near + y
    ends = (z == 0) | (z == last)
    chunks = local // CHUNK

    barrier = pltpu.get_barrier_semaphore()
    for k in range(1, count):
        pl.semaphore_signal(barrier, inc=1, device_id={"trn": lax.rem(me + k, count)})

    def fetch(index, source, target):
        return pltpu.make_async_copy(source, target, in_sems.at[index])

    fetch_train = fetch(0, train_hbm, train_ref)
    fetch_test = fetch(1, test_hbm, test_ref)
    fetch_weights = fetch(2, weights_hbm, weights_ref)

    def fetch_factor(index):
        block = pl.ds(index * CHUNK, CHUNK)
        return fetch(3 + index, factor_hbm.at[block], factor_ref.at[block])

    fetch_train.start()
    fetch_test.start()
    fetch_weights.start()
    for index in range(chunks):
        fetch_factor(index).start()

    var_acc[...] = jnp.zeros_like(var_acc)
    fetch_train.wait()

    def prepare_train(index, carry):
        cols = pl.ds(pl.multiple_of(index * 512, 512), 512)
        points = train_ref[:, cols]
        squares = points.astype(jnp.float32) ** 2
        norm = jnp.sum(squares, axis=0, keepdims=True) * (-4.0 / dim)
        high, middle, low = pieces(norm)
        row = lax.broadcasted_iota(jnp.int32, (16, 512), 0)
        one = jnp.float32(1.0)
        extra = pick(row, ((0, one), (1, one), (2, one), (3, high), (4, middle), (5, low)), jnp.float32(0.0))
        train_aug[:dim, cols] = points
        train_aug[dim : dim + 16, cols] = extra.astype(jnp.bfloat16)
        train_aug[dim + 16 :, cols] = jnp.zeros((depth - dim - 16, 512), jnp.bfloat16)
        return carry

    lax.fori_loop(0, local // 512, prepare_train, 0)
    fetch_test.wait()

    def prepare_test(index, carry):
        cols = pl.ds(pl.multiple_of(index * 256, 256), 256)
        points = test_ref[:, cols].astype(jnp.float32)
        norm = jnp.sum(points * points, axis=0, keepdims=True) * (-4.0 / dim)
        high, middle, low = pieces(norm)
        row = lax.broadcasted_iota(jnp.int32, (8, 256), 0)
        one = jnp.float32(1.0)
        extra = pick(row, ((0, high), (1, middle), (2, low), (3, one), (4, one), (5, one)), jnp.float32(0.0))
        whole = jnp.concatenate(
            [points * (8.0 / dim), extra, jnp.zeros((depth - dim - 8, 256), jnp.float32)], axis=0
        )
        test_aug[cols, :] = whole.T
        return carry

    lax.fori_loop(0, rows // 256, prepare_test, 0)
    fetch_weights.wait()
    for index in range(local // 128):
        wide[:, index * 128 : (index + 1) * 128] = weights_ref[index : index + 1, :].astype(jnp.float32)

    def edge_places(kind, step):
        begin, number, gb, ga, base = kind
        index = step - begin

        def row_of(who, early):
            inner = base + (number * gb + index * ga if early else index * gb)
            return pl.multiple_of(who * span + inner, 8)

        where = (
            row_of(far, False), row_of(far + 1, False), row_of(near, False), row_of(near + 1, False),
            row_of(far + 1 - y, True), row_of(near + 1 - y, True), row_of(far + y, True), row_of(near + y, True),
        )
        return tuple(zip(where, (gb,) * 4 + (ga,) * 4))

    def middle_places(step):
        begin, _, gm, base = middle
        inner = base + (step - begin) * gm
        who = (far + 1 - y, near + 1 - y, far + y, near + y)
        return tuple((pl.multiple_of(w * span + inner, 8), gm) for w in who)

    layouts = [(kind[0], kind[1], functools.partial(edge_places, kind)) for kind in kinds]
    layouts.append((middle[0], middle[1], middle_places))

    def compute(step, first=False):
        for begin, number, places in layouts:
            if first and begin > 0:
                continue

            def gather():
                left_ref[...] = jnp.concatenate(
                    [test_aug[pl.ds(at, size), :] for at, size in places(step)], axis=0
                ).astype(jnp.bfloat16)

            if first:
                gather()
            else:
                pl.when((step >= begin) & (step < begin + number))(gather)
        left = left_ref[...]
        total = None
        means = None
        for index in range(chunks):
            begin = index * CHUNK
            power = jnp.dot(
                left, train_aug[:, begin : begin + CHUNK], preferred_element_type=jnp.float32
            )
            values = jnp.exp2(power * LOG2E).astype(jnp.bfloat16)
            scaled = values.astype(jnp.float32) * wide[:, begin : begin + CHUNK]
            for lane in range(0, CHUNK, 128):
                piece = scaled[:, lane : lane + 128]
                means = piece if means is None else means + piece
            if first:
                fetch_factor(index).wait()
            product = jnp.dot(
                values, factor_ref[begin : begin + CHUNK, :], preferred_element_type=jnp.float32
            )
            total = product if total is None else total + product
        part[step] = total
        mean_acc[pl.ds(pl.multiple_of(step * BLOCK, BLOCK), BLOCK), :] = means

    def send(source, target, ssem, rsem, device):
        return pltpu.make_async_remote_copy(
            src_ref=source, dst_ref=target, send_sem=ssem, recv_sem=rsem, device_id={"trn": device}
        )

    def square(values):
        total = None
        for lane in range(0, values.shape[1], 128):
            piece = values[:, lane : lane + 128]
            total = piece * piece if total is None else total + piece * piece
        return total

    class Kind:
        def __init__(self, kind, buffers):
            self.begin, self.number, self.gb, self.ga, self.base = kind
            self.got_y, self.bp, self.bq, self.ap, self.aq, self.got_x = buffers
            gb, ga = self.gb, self.ga
            self.sent = slice(4 * gb, 4 * gb + 2 * ga)
            self.kept = slice(4 * gb + 2 * ga, 4 * gb + 4 * ga)
            self.out_b, self.in_b = slice(0, 2 * gb), slice(2 * gb, 4 * gb)
            self.out_a = slice(4 * gb + 2 * ga, 4 * gb + 3 * ga)
            self.in_a = slice(4 * gb + 3 * ga, 4 * gb + 4 * ga)

        def has(self, s):
            return (s >= self.begin) & (s < self.begin + self.number)

        def copy_y(self, s):
            return send(part.at[s, self.sent], self.got_y.at[s - self.begin], s_y.at[s], r_y.at[s], other)

        def first_b(self, s):
            return send(part.at[s, self.out_b], self.bp.at[s - self.begin], s_b.at[s], rp_b.at[s], toward)

        def cross_b(self, s):
            j = s - self.begin
            return send(self.bp.at[j], self.bq.at[j], s_b.at[s], rq_b.at[s], toward)

        def back_b(self, s):
            j = s - self.begin
            return send(self.bq.at[j], self.bq.at[j], sq_b.at[s], rq_b.at[s], back)

        def first_a(self, s):
            return send(part.at[s, self.out_a], self.ap.at[s - self.begin], s_a.at[s], rp_a.at[s], toward)

        def cross_a(self, s):
            j = s - self.begin
            return send(self.ap.at[j], self.aq.at[j], s_a.at[s], rq_a.at[s], toward)

        def back_a(self, s):
            j = s - self.begin
            return send(self.aq.at[j], self.aq.at[j], sq_a.at[s], rq_a.at[s], back)

        def swap(self, s):
            j = s - self.begin
            theirs = pl.ds(pl.multiple_of((1 - y) * self.gb, 8), self.gb)
            return send(self.bq.at[j, theirs], self.got_x.at[j], s_x.at[s], r_x.at[s], other)

    table = [Kind(kind, got[6 * i : 6 * i + 6]) for i, kind in enumerate(kinds)]
    m_begin, m_number, gm, m_base = middle

    def m_has(s):
        return (s >= m_begin) & (s < m_begin + m_number)

    def m_y(s):
        j = s - m_begin
        return (
            send(part.at[s, :gm], got_yf.at[j], s_y.at[s], r_y.at[s], other),
            send(part.at[s, gm : 2 * gm], got_yn.at[j], s_yn.at[j], r_yn.at[j], other),
        )

    def m_first(s):
        j = s - m_begin
        return (
            send(part.at[s, 2 * gm : 3 * gm], got_mf.at[j], s_mf.at[j], r_mf.at[j], toward),
            send(part.at[s, 3 * gm :], got_mn.at[j], s_mn.at[j], r_mn.at[j], toward),
        )

    def m_cross(s):
        j = s - m_begin
        return send(got_mf.at[j], got_mx.at[j], s_mx.at[j], r_mx.at[j], toward)

    def mean_swap():
        return send(mean_box.at[z], mean_box.at[LINE], s_mean.at[0], r_mean.at[0], other)

    def mean_copy(k):
        target = lax.rem(me + k * pair, count)
        return send(mean_box.at[z], mean_box.at[z], s_mean.at[k], r_mean.at[k], target)

    def mean_start():
        for begin, number, places in layouts:
            def place(step, carry):
                start = pl.multiple_of(step * BLOCK, BLOCK)
                for at, size in places(step):
                    test_aug[pl.ds(at, size), :] = mean_acc[pl.ds(start, size), :]
                    start = pl.multiple_of(start + size, 8)
                return carry

            lax.fori_loop(begin, begin + number, place, 0)
        for index in range(rows // 128):
            block = test_aug[index * 128 : (index + 1) * 128, :]
            mean_box[z, index : index + 1, :] = jnp.sum(block.T, axis=0, keepdims=True)
        mean_swap().start()

    def mean_spread():
        mean_swap().wait()
        mean_box[z] = mean_box[z] + mean_box[LINE]
        for k in range(1, LINE):
            mean_copy(k).start()

    lines = span // 128

    def line_of(index):
        block = var_acc[index * 128 : (index + 1) * 128, :]
        return jnp.sum(block.T, axis=0, keepdims=True)

    def var_copy(k, who):
        return send(var_box.at[who], var_box.at[who], s_var.at[k], r_var.at[who], lax.rem(me + k, count))

    def mid_copy(k, who):
        return send(mid_box.at[who], mid_box.at[who], s_var.at[k], r_mid.at[who], lax.rem(me + k, count))

    def receive_y(it):
        for kind in table:
            s = it - LAG_Y

            @pl.when(kind.has(s))
            def _():
                kind.copy_y(s).wait_recv()
                part[s, kind.kept] = part[s, kind.kept] + kind.got_y[s - kind.begin]

    def receive_m(s):
        j = s - m_begin
        yf, yn = m_y(s)
        yf.wait_recv()
        part[s, 2 * gm : 3 * gm] = part[s, 2 * gm : 3 * gm] + got_yf[j]
        yield
        yn.wait_recv()
        part[s, 3 * gm :] = part[s, 3 * gm :] + got_yn[j]

    def send_y(it):
        for kind in table:
            pl.when(kind.has(it))(lambda: kind.copy_y(it).start())

        @pl.when(m_has(it))
        def _():
            for copy in m_y(it):
                copy.start()

    def means(it):
        pl.when(it == steps + MEAN_AT)(mean_start)
        pl.when(it == steps + MEAN_ON)(mean_spread)

    def end_turn(it, carry):
        pl.when((it > 0) & (it < steps))(lambda: compute(it))
        for kind in table:
            pl.when(kind.has(it))(lambda: kind.first_b(it).start())
        send_y(it)
        for kind in table:
            s_hold = it - LAG_B[3]

            @pl.when(kind.has(s_hold))
            def _():
                kind.back_b(s_hold).wait_recv()
                j = s_hold - kind.begin
                kind.bq[j] = kind.bq[j] + part[s_hold, kind.in_b]

        receive_y(it)
        for kind in table:
            s_go = it - LAG_A[0]
            pl.when(kind.has(s_go))(lambda: kind.first_a(s_go).start())
        s_m = it - LAG_M[0]

        @pl.when(m_has(s_m))
        def _():
            mf, mn = m_first(s_m)
            waits = receive_m(s_m)
            next(waits)
            mf.start()
            next(waits, None)
            mn.start()

        for kind in table:
            gb, ga = kind.gb, kind.ga
            s_a3, s_swap, s_last = it - LAG_A[3], it - LAG_SWAP, it - LAG_X

            @pl.when(kind.has(s_a3))
            def _():
                kind.back_a(s_a3).wait_recv()
                j = s_a3 - kind.begin
                at = pl.multiple_of(kind.base + gb * kind.number + j * ga, 8)
                var_acc[pl.ds(at, ga), :] = square(kind.aq[j] + part[s_a3, kind.in_a])

            pl.when(kind.has(s_swap))(lambda: kind.swap(s_swap).start())

            @pl.when(kind.has(s_last))
            def _():
                kind.swap(s_last).wait_recv()
                j = s_last - kind.begin
                mine = pl.ds(pl.multiple_of(y * gb, 8), gb)
                at = pl.multiple_of(kind.base + j * gb, 8)
                var_acc[pl.ds(at, gb), :] = square(kind.bq[j, mine] + kind.got_x[j])

        means(it)
        return carry

    def middle_turn(it, carry):
        pl.when((it > 0) & (it < steps))(lambda: compute(it))
        send_y(it)
        for kind in table:
            s_1, s_2 = it - LAG_B[1], it - LAG_B[2]

            @pl.when(kind.has(s_1))
            def _():
                kind.first_b(s_1).wait_recv()
                j = s_1 - kind.begin
                kind.bp[j] = kind.bp[j] + part[s_1, kind.out_b]
                kind.cross_b(s_1).start()

            @pl.when(kind.has(s_2))
            def _():
                kind.cross_b(s_2).wait_recv()
                j = s_2 - kind.begin
                kind.bq[j] = kind.bq[j] + part[s_2, kind.in_b]
                kind.back_b(s_2).start()

        receive_y(it)
        s_m = it - LAG_M[0]

        @pl.when(m_has(s_m))
        def _():
            for _ in receive_m(s_m):
                pass

        for kind in table:
            s_1, s_2 = it - LAG_A[1], it - LAG_A[2]

            @pl.when(kind.has(s_1))
            def _():
                kind.first_a(s_1).wait_recv()
                j = s_1 - kind.begin
                kind.ap[j] = kind.ap[j] + part[s_1, kind.out_a]
                kind.cross_a(s_1).start()

            @pl.when(kind.has(s_2))
            def _():
                kind.cross_a(s_2).wait_recv()
                j = s_2 - kind.begin
                kind.aq[j] = kind.aq[j] + part[s_2, kind.in_a]
                kind.back_a(s_2).start()

        s_m1, s_m2 = it - LAG_M[1], it - LAG_M[2]

        @pl.when(m_has(s_m1))
        def _():
            m_first(s_m1)[0].wait_recv()
            j = s_m1 - m_begin
            got_mf[j] = got_mf[j] + part[s_m1, 2 * gm : 3 * gm]
            m_cross(s_m1).start()

        @pl.when(m_has(s_m2))
        def _():
            m_first(s_m2)[1].wait_recv()
            m_cross(s_m2).wait_recv()
            j = s_m2 - m_begin
            at = pl.multiple_of(m_base + j * gm, 8)
            var_acc[pl.ds(at, gm), :] = square(got_mn[j] + part[s_m2, 3 * gm :] + got_mx[j])

        means(it)
        return carry

    def settle_y():
        for kind in table:
            def done(s, carry):
                kind.copy_y(s).wait_send()
                return carry

            lax.fori_loop(kind.begin, kind.begin + kind.number, done, 0)

        for s in range(m_begin, m_begin + m_number):
            for copy in m_y(s):
                copy.wait_send()

    def collect(is_end):
        for k in range(1, LINE):
            mean_copy(k).wait()
        total = mean_box[0]
        for index in range(1, LINE):
            total = total + mean_box[index]
        out_ref[: rows // 128, :] = total
        settle_y()
        for kind in table:
            def done(s, carry):
                if is_end:
                    for copy in (kind.first_b(s), kind.first_a(s), kind.swap(s)):
                        copy.wait_send()
                else:
                    for copy in (kind.cross_b(s), kind.back_b(s), kind.cross_a(s), kind.back_a(s)):
                        copy.wait_send()
                return carry

            lax.fori_loop(kind.begin, kind.begin + kind.number, done, 0)
        for s in range(m_begin, m_begin + m_number):
            for copy in m_first(s) if is_end else (m_cross(s),):
                copy.wait_send()
        for who in range(4):
            if is_end:
                mid_copy(1, who).wait_recv()
                pl.when(owner != who)(lambda: var_copy(1, who).wait_recv())
            else:
                var_copy(1, who).wait_recv()
                pl.when(owner != who)(lambda: mid_copy(1, who).wait_recv())
        for who in range(4):
            begin = rows // 128 + who * lines
            out_ref[begin : begin + lines - 1, :] = 1.0 - var_box[who, : lines - 1]
            out_ref[begin + lines - 1 : begin + lines, :] = 1.0 - (var_box[who, lines - 1 :] + mid_box[who])
        for k in range(1, count):
            (var_copy if is_end else mid_copy)(k, owner).wait_send()

    compute(0, True)
    pl.semaphore_wait(barrier, count - 1)
    total_turns = steps + max(LAG_X, LAG_A[3], LAG_M[2])

    @pl.when(ends)
    def _():
        lax.fori_loop(0, total_turns, end_turn, 0)
        for index in range(lines):
            var_box[owner, index : index + 1, :] = line_of(index)
        for k in range(1, count):
            var_copy(k, owner).start()
        collect(True)

    @pl.when(jnp.logical_not(ends))
    def _():
        lax.fori_loop(0, total_turns, middle_turn, 0)
        mid_box[owner] = line_of(lines - 1)
        for k in range(1, count):
            mid_copy(k, owner).start()
        collect(False)


def fused(test_points, train_points, weights, factor, *, count):
    dim, rows = test_points.shape
    local = train_points.shape[1]
    width = factor.shape[1]
    depth = -(-(dim + 16) // 128) * 128
    steps = rows // BLOCK
    dma = pltpu.SemaphoreType.DMA
    f32 = jnp.float32
    kinds, (_, m_number, gm, _) = kinds_of(rows)
    sems = [dma((steps,))] * 12 + [dma((m_number,))] * 8
    sems += [dma((LINE,)), dma((LINE,)), dma((count,)), dma((4,)), dma((4,))]
    boxes = [pltpu.VMEM((m_number, gm, width), f32)] * 5
    for _, number, gb, ga, _ in kinds:
        for size in (2 * ga, 2 * gb, 2 * gb, ga, ga, gb):
            boxes.append(pltpu.VMEM((number, size, width), f32))
    out = pl.pallas_call(
        functools.partial(kernel, count=count),
        out_shape=jax.ShapeDtypeStruct((rows // 64, 128), f32),
        in_specs=[pl.BlockSpec(memory_space=pl.ANY)] * 4,
        out_specs=pl.BlockSpec(memory_space=pltpu.VMEM),
        scratch_shapes=[
            pltpu.VMEM((dim, rows), jnp.bfloat16),
            pltpu.VMEM((dim, local), jnp.bfloat16),
            pltpu.VMEM((local // 128, 128), jnp.bfloat16),
            pltpu.VMEM((local, width), jnp.bfloat16),
            dma((3 + local // CHUNK,)),
            pltpu.VMEM((rows, depth), f32),
            pltpu.VMEM((depth, local), jnp.bfloat16),
            pltpu.VMEM((1, local), f32),
            pltpu.VMEM((BLOCK, depth), jnp.bfloat16),
            pltpu.VMEM((steps, BLOCK, width), f32),
            pltpu.VMEM((rows, 128), f32),
            pltpu.VMEM((rows // 4, 128), f32),
            pltpu.VMEM((LINE + 1, rows // 128, 128), f32),
            pltpu.VMEM((4, rows // 512, 128), f32),
            pltpu.VMEM((4, 1, 128), f32),
        ] + sems + boxes,
        compiler_params=pltpu.CompilerParams(
            collective_id=0, has_side_effects=True, vmem_limit_bytes=56 * 1024 * 1024
        ),
    )(test_points, train_points, weights.reshape(local // 128, 128), factor)
    lines = rows // 128
    return out[:lines].reshape(rows), out[lines:].reshape(rows)


def on_device(test_points, train_points, weights, factor):
    rows = test_points.shape[1]
    local = train_points.shape[1]
    dim = test_points.shape[0]
    width = factor.shape[1]
    test_sq = jnp.sum(test_points.astype(jnp.float32) ** 2, axis=0)
    block = math.gcd(local, 1024)
    turns = local // block

    def step(index, carry):
        mean_acc, proj_acc = carry
        start = (index * block).astype(jnp.int32)
        points = lax.dynamic_slice_in_dim(train_points, start, block, 1)
        wblock = lax.dynamic_slice_in_dim(weights, start, block, 0)
        fblock = lax.dynamic_slice_in_dim(factor, start, block, 0)
        train_sq = jnp.sum(points.astype(jnp.float32) ** 2, axis=0)
        cross = lax.dot_general(
            test_points, points, (((0,), (0,)), ((), ())), preferred_element_type=jnp.float32
        )
        kernel = jnp.exp(
            -(test_sq[:, None] + train_sq[None, :] - 2.0 * cross) * (4.0 / dim)
        ).astype(jnp.bfloat16)
        mean_acc = mean_acc + jnp.dot(kernel, wblock, preferred_element_type=jnp.float32)
        proj_acc = proj_acc + jnp.dot(kernel, fblock, preferred_element_type=jnp.float32)
        return (mean_acc, proj_acc)

    init = (jnp.zeros((rows,), jnp.float32), jnp.zeros((rows, width), jnp.float32))
    mean_part, proj_part = lax.fori_loop(0, turns, step, init)
    mean_share, proj_share = (
        lax.psum_scatter(mean_part, "trn", scatter_dimension=0, tiled=True),
        lax.psum_scatter(proj_part, "trn", scatter_dimension=0, tiled=True),
    )
    var_share = 1.0 - jnp.sum(proj_share * proj_share, axis=1)
    mean, variance = (
        lax.all_gather(mean_share, "trn", axis=0, tiled=True),
        lax.all_gather(var_share, "trn", axis=0, tiled=True),
    )
    return (mean, variance)


def solution(mesh):
    in_specs = (
        P(None, ("grp", "tst")),
        P(None, ("grp", "trn")),
        P(("grp", "trn")),
        P(("grp", "trn"), None),
    )
    out_specs = (P(("grp", "tst")), P(("grp", "tst")))
    count = mesh.shape["trn"]
    body = functools.partial(fused, count=count) if count == 2 * LINE else on_device
    return jax.shard_map(
        body, mesh=mesh, in_specs=in_specs, out_specs=out_specs, check_vma=False
    )
```

time: 58.5 us -> 56.3 us (0.962)
  Pallas kernels: 56.3 us -> 54.1 us
    pallas_call x1, Pallas kernels: 56.3 us -> 54.1 us  [fused(): pl.pallas_call(functools.partial(kernel, count=count), out_shape=jax.Shap...]
where the time goes in v2:
time: 56.3 us; the launch traced here: 56.1 us
  Pallas kernels  54.1 us (96%)
  local copies, waits for them, and re-layouts  1.32 us (2%)
  between operations  0.64 us (1%)
    pallas_call x1, Pallas kernels, fused(): pl.pallas_call(functools.partial(kernel, count=count), out_shape=jax.Shap...  54.1 us
    reshape x1, local copies, waits for them, and re-layouts, fused(): return (out[:lines].reshape(rows), out[lines:].reshape(rows))  1.32 us

profile of v2, /device:TPU:0, one launch (start us, length us, event | category | flops | bytes accessed | tf_op | source)
XLA Modules:
  0.0 56.1 jit_solution(4032722970866828392)
XLA Ops:
  0.6 54.1 %shard_map.59 = f32[32,128]{1,0:T(8,128)} custom-call(bf16[64,2048]{1,0:T(8,128)(2,1)} %test_hbm.1, bf16[64,4096]{1,0:T(8,128)(2,1)} %train_hbm.1, bf16[32,128]{1,0:T(8,128)(2,1)} %bitcast.5, bf16[4096,512]{1,0:T(8,128)(2,1)} %factor_hbm.1), custom_call_target="tpu_custom_call" | custom-call | tf_op jit(solution)/shard_map/pallas_call | solution.py:555
  54.8 1.3 %slice_bitcast_fusion = (f32[2048]{0:T(1024)}, f32[2048]{0:T(1024)}) fusion(f32[32,128]{1,0:T(8,128)} %shard_map.59), kind=kLoop, calls=%fused_computation | loop fusion | bytes 32768 | tf_op jit(solution)/shard_map/reshape | solution.py:582

commit v3 on v2

--- a/solution.py
+++ b/solution.py
@@ -52,7 +52,7 @@
 
 def kernel(
     test_hbm, train_hbm, weights_hbm, factor_hbm, out_ref,
-    test_ref, train_ref, weights_ref, factor_ref, in_sems,
+    test_ref, weights_ref, factor_ref, in_sems,
     test_aug, train_aug, wide, left_ref, part, mean_acc, var_acc, mean_box, var_box, mid_box,
     s_y, r_y, s_b, rp_b, sq_b, rq_b, s_a, rp_a, sq_a, rq_a, s_x, r_x,
     s_yn, r_yn, s_mf, r_mf, s_mn, r_mn, s_mx, r_mx,
@@ -64,7 +64,7 @@
     z = me // pair
     y = me % pair
     dim, rows = test_ref.shape
-    local = train_ref.shape[1]
+    local = train_aug.shape[1]
     depth = test_aug.shape[1]
     steps = rows // BLOCK
     kinds, middle = kinds_of(rows)
@@ -86,7 +86,7 @@
     def fetch(index, source, target):
         return pltpu.make_async_copy(source, target, in_sems.at[index])
 
-    fetch_train = fetch(0, train_hbm, train_ref)
+    fetch_train = fetch(0, train_hbm, train_aug.at[:dim])
     fetch_test = fetch(1, test_hbm, test_ref)
     fetch_weights = fetch(2, weights_hbm, weights_ref)
 
@@ -101,23 +101,22 @@
         fetch_factor(index).start()
 
     var_acc[...] = jnp.zeros_like(var_acc)
+    train_aug[dim + 16 :, :] = jnp.zeros((depth - dim - 16, local), jnp.bfloat16)
     fetch_train.wait()
 
     def prepare_train(index, carry):
         cols = pl.ds(pl.multiple_of(index * 512, 512), 512)
-        points = train_ref[:, cols]
+        points = train_aug[:dim, cols]
         squares = points.astype(jnp.float32) ** 2
         norm = jnp.sum(squares, axis=0, keepdims=True) * (-4.0 / dim)
         high, middle, low = pieces(norm)
         row = lax.broadcasted_iota(jnp.int32, (16, 512), 0)
         one = jnp.float32(1.0)
         extra = pick(row, ((0, one), (1, one), (2, one), (3, high), (4, middle), (5, low)), jnp.float32(0.0))
-        train_aug[:dim, cols] = points
         train_aug[dim : dim + 16, cols] = extra.astype(jnp.bfloat16)
-        train_aug[dim + 16 :, cols] = jnp.zeros((depth - dim - 16, 512), jnp.bfloat16)
         return carry
 
-    lax.fori_loop(0, local // 512, prepare_train, 0)
+    lax.fori_loop(0, local // 512, prepare_train, 0, unroll=True)
     fetch_test.wait()
 
     def prepare_test(index, carry):
@@ -189,8 +188,6 @@
             for lane in range(0, CHUNK, 128):
                 piece = scaled[:, lane : lane + 128]
                 means = piece if means is None else means + piece
-            if first:
-                fetch_factor(index).wait()
             product = jnp.dot(
                 values, factor_ref[begin : begin + CHUNK, :], preferred_element_type=jnp.float32
             )
@@ -515,6 +512,8 @@
         for k in range(1, count):
             (var_copy if is_end else mid_copy)(k, owner).wait_send()
 
+    for index in range(chunks):
+        fetch_factor(index).wait()
     compute(0, True)
     pl.semaphore_wait(barrier, count - 1)
     total_turns = steps + max(LAG_X, LAG_A[3], LAG_M[2])
@@ -554,12 +553,11 @@
             boxes.append(pltpu.VMEM((number, size, width), f32))
     out = pl.pallas_call(
         functools.partial(kernel, count=count),
-        out_shape=jax.ShapeDtypeStruct((rows // 64, 128), f32),
+        out_shape=pltpu.VMEM((rows // 64, 128), f32),
         in_specs=[pl.BlockSpec(memory_space=pl.ANY)] * 4,
         out_specs=pl.BlockSpec(memory_space=pltpu.VMEM),
         scratch_shapes=[
             pltpu.VMEM((dim, rows), jnp.bfloat16),
-            pltpu.VMEM((dim, local), jnp.bfloat16),
             pltpu.VMEM((local // 128, 128), jnp.bfloat16),
             pltpu.VMEM((local, width), jnp.bfloat16),
             dma((3 + local // CHUNK,)),
@@ -575,9 +573,9 @@
             pltpu.VMEM((4, 1, 128), f32),
         ] + sems + boxes,
         compiler_params=pltpu.CompilerParams(
-            collective_id=0, has_side_effects=True, vmem_limit_bytes=56 * 1024 * 1024
+            collective_id=0, has_side_effects=True, vmem_limit_bytes=40 * 1024 * 1024
         ),
-    )(test_points, train_points, weights.reshape(local // 128, 128), factor)
+    )(*[pltpu.with_memory_space_constraint(x, pltpu.HBM) for x in (test_points, train_points, weights.reshape(local // 128, 128), factor)])
     lines = rows // 128
     return out[:lines].reshape(rows), out[lines:].reshape(rows)
 

time: 56.3 us -> 54.5 us (0.968)
  Pallas kernels: 54.1 us -> 53.1 us
  local copies, waits for them, and re-layouts: 1.32 us -> 0.61 us
    pallas_call x1, Pallas kernels: 54.1 us -> 53.1 us  [fused(): pl.pallas_call(functools.partial(kernel, count=count), out_shape=pltpu.VM...]
    reshape x1, local copies, waits for them, and re-layouts: 1.32 us -> 0.61 us  [fused(): return (out[:lines].reshape(rows), out[lines:].reshape(rows))]
where the time goes in v3:
time: 54.5 us; the launch traced here: 54.4 us
  Pallas kernels  53.1 us (97%)
  between operations  0.64 us (1%)
  local copies, waits for them, and re-layouts  0.61 us (1%)
    pallas_call x1, Pallas kernels, fused(): pl.pallas_call(functools.partial(kernel, count=count), out_shape=pltpu.VM...  53.1 us

profile of v3, /device:TPU:0, one launch (start us, length us, event | category | flops | bytes accessed | tf_op | source)
XLA Modules:
  0.0 54.4 jit_solution(12537105753546076185)
XLA Ops:
  0.6 53.1 %shard_map.59 = f32[32,128]{1,0:T(8,128)S(1)} custom-call(bf16[64,2048]{1,0:T(8,128)(2,1)} %test_hbm.1, bf16[64,4096]{1,0:T(8,128)(2,1)} %train_hbm.1, bf16[32,128]{1,0:T(8,128)(2,1)} %bitcast.5, bf16[4096,512]{1,0:T(8,128)(2,1)} %factor_hbm.1), custom_call_target="tpu_custom_call" | custom-call | tf_op jit(solution)/shard_map/pallas_call | solution.py:554
  53.8 0.6 %slice_bitcast_fusion = (f32[2048]{0:T(1024)}, f32[2048]{0:T(1024)}) fusion(f32[32,128]{1,0:T(8,128)S(1)} %shard_map.59), kind=kLoop, calls=%fused_computation | loop fusion | bytes 32768 | tf_op jit(solution)/shard_map/reshape | solution.py:580

commit v4 on v3

--- a/solution.py
+++ b/solution.py
@@ -79,10 +79,6 @@
     ends = (z == 0) | (z == last)
     chunks = local // CHUNK
 
-    barrier = pltpu.get_barrier_semaphore()
-    for k in range(1, count):
-        pl.semaphore_signal(barrier, inc=1, device_id={"trn": lax.rem(me + k, count)})
-
     def fetch(index, source, target):
         return pltpu.make_async_copy(source, target, in_sems.at[index])
 
@@ -99,6 +95,10 @@
     fetch_weights.start()
     for index in range(chunks):
         fetch_factor(index).start()
+
+    barrier = pltpu.get_barrier_semaphore()
+    for k in range(1, count):
+        pl.semaphore_signal(barrier, inc=1, device_id={"trn": lax.rem(me + k, count)})
 
     var_acc[...] = jnp.zeros_like(var_acc)
     train_aug[dim + 16 :, :] = jnp.zeros((depth - dim - 16, local), jnp.bfloat16)
@@ -133,7 +133,7 @@
         test_aug[cols, :] = whole.T
         return carry
 
-    lax.fori_loop(0, rows // 256, prepare_test, 0)
+    lax.fori_loop(0, rows // 256, prepare_test, 0, unroll=True)
     fetch_weights.wait()
     for index in range(local // 128):
         wide[:, index * 128 : (index + 1) * 128] = weights_ref[index : index + 1, :].astype(jnp.float32)
@@ -178,6 +178,7 @@
         left = left_ref[...]
         total = None
         means = None
+        held = []
         for index in range(chunks):
             begin = index * CHUNK
             power = jnp.dot(
@@ -188,10 +189,19 @@
             for lane in range(0, CHUNK, 128):
                 piece = scaled[:, lane : lane + 128]
                 means = piece if means is None else means + piece
+            if first:
+                held.append(values)
+                continue
             product = jnp.dot(
                 values, factor_ref[begin : begin + CHUNK, :], preferred_element_type=jnp.float32
             )
             total = product if total is None else total + product
+        if first:
+            for index in range(chunks):
+                fetch_factor(index).wait()
+            total = jnp.dot(
+                jnp.concatenate(held, axis=1), factor_ref[...], preferred_element_type=jnp.float32
+            )
         part[step] = total
         mean_acc[pl.ds(pl.multiple_of(step * BLOCK, BLOCK), BLOCK), :] = means
 
@@ -512,8 +522,6 @@
         for k in range(1, count):
             (var_copy if is_end else mid_copy)(k, owner).wait_send()
 
-    for index in range(chunks):
-        fetch_factor(index).wait()
     compute(0, True)
     pl.semaphore_wait(barrier, count - 1)
     total_turns = steps + max(LAG_X, LAG_A[3], LAG_M[2])

time: 54.5 us -> 53.8 us (0.987)
  Pallas kernels: 53.1 us -> 52.4 us
    pallas_call x1, Pallas kernels: 53.1 us -> 52.4 us  [fused(): pl.pallas_call(functools.partial(kernel, count=count), out_shape=pltpu.VM...]
where the time goes in v4:
time: 53.8 us; the launch traced here: 53.7 us
  Pallas kernels  52.4 us (97%)
  between operations  0.64 us (1%)
  local copies, waits for them, and re-layouts  0.61 us (1%)
    pallas_call x1, Pallas kernels, fused(): pl.pallas_call(functools.partial(kernel, count=count), out_shape=pltpu.VM...  52.4 us

profile of v4, /device:TPU:0, one launch (start us, length us, event | category | flops | bytes accessed | tf_op | source)
XLA Modules:
  0.0 53.7 jit_solution(18055641260789480150)
XLA Ops:
  0.6 52.4 %shard_map.59 = f32[32,128]{1,0:T(8,128)S(1)} custom-call(bf16[64,2048]{1,0:T(8,128)(2,1)} %test_hbm.1, bf16[64,4096]{1,0:T(8,128)(2,1)} %train_hbm.1, bf16[32,128]{1,0:T(8,128)(2,1)} %bitcast.5, bf16[4096,512]{1,0:T(8,128)(2,1)} %factor_hbm.1), custom_call_target="tpu_custom_call" | custom-call | tf_op jit(solution)/shard_map/pallas_call | solution.py:562
  53.1 0.6 %slice_bitcast_fusion = (f32[2048]{0:T(1024)}, f32[2048]{0:T(1024)}) fusion(f32[32,128]{1,0:T(8,128)S(1)} %shard_map.59), kind=kLoop, calls=%fused_computation | loop fusion | bytes 32768 | tf_op jit(solution)/shard_map/reshape | solution.py:588

commit v5 on v4

--- a/solution.py
+++ b/solution.py
@@ -361,6 +361,10 @@
         for kind in table:
             pl.when(kind.has(it))(lambda: kind.first_b(it).start())
         send_y(it)
+        receive_y(it)
+        for kind in table:
+            s_go = it - LAG_A[0]
+            pl.when(kind.has(s_go))(lambda: kind.first_a(s_go).start())
         for kind in table:
             s_hold = it - LAG_B[3]
 
@@ -370,10 +374,6 @@
                 j = s_hold - kind.begin
                 kind.bq[j] = kind.bq[j] + part[s_hold, kind.in_b]
 
-        receive_y(it)
-        for kind in table:
-            s_go = it - LAG_A[0]
-            pl.when(kind.has(s_go))(lambda: kind.first_a(s_go).start())
         s_m = it - LAG_M[0]
 
         @pl.when(m_has(s_m))

time: 53.8 us -> 53.8 us (level)
  no operation moved by 1% of the time
where the time goes in v5:
time: 53.8 us; the launch traced here: 53.7 us
  Pallas kernels  52.4 us (97%)
  between operations  0.64 us (1%)
  local copies, waits for them, and re-layouts  0.61 us (1%)
    pallas_call x1, Pallas kernels, fused(): pl.pallas_call(functools.partial(kernel, count=count), out_shape=pltpu.VM...  52.4 us

profile of v5, /device:TPU:0, one launch (start us, length us, event | category | flops | bytes accessed | tf_op | source)
XLA Modules:
  0.0 53.7 jit_solution(16945671364836223555)
XLA Ops:
  0.6 52.4 %shard_map.59 = f32[32,128]{1,0:T(8,128)S(1)} custom-call(bf16[64,2048]{1,0:T(8,128)(2,1)} %test_hbm.1, bf16[64,4096]{1,0:T(8,128)(2,1)} %train_hbm.1, bf16[32,128]{1,0:T(8,128)(2,1)} %bitcast.5, bf16[4096,512]{1,0:T(8,128)(2,1)} %factor_hbm.1), custom_call_target="tpu_custom_call" | custom-call | tf_op jit(solution)/shard_map/pallas_call | solution.py:562
  53.1 0.6 %slice_bitcast_fusion = (f32[2048]{0:T(1024)}, f32[2048]{0:T(1024)}) fusion(f32[32,128]{1,0:T(8,128)S(1)} %shard_map.59), kind=kLoop, calls=%fused_computation | loop fusion | bytes 32768 | tf_op jit(solution)/shard_map/reshape | solution.py:588

commit v6 on v4

--- a/solution.py
+++ b/solution.py
@@ -19,7 +19,7 @@
 LAG_A = (3, 5, 8, 18)
 LAG_SWAP = 11
 LAG_X = 18
-LAG_M = (4, 6, 17)
+LAG_M = (4, 6, 14)
 MEAN_AT = 1
 MEAN_ON = 4
 

time: 53.8 us -> 53.8 us (level)
  no operation moved by 1% of the time
where the time goes in v6:
time: 53.8 us; the launch traced here: 53.7 us
  Pallas kernels  52.4 us (97%)
  between operations  0.64 us (1%)
  local copies, waits for them, and re-layouts  0.61 us (1%)
    pallas_call x1, Pallas kernels, fused(): pl.pallas_call(functools.partial(kernel, count=count), out_shape=pltpu.VM...  52.4 us

profile of v6, /device:TPU:0, one launch (start us, length us, event | category | flops | bytes accessed | tf_op | source)
XLA Modules:
  0.0 53.7 jit_solution(4071494956903235890)
XLA Ops:
  0.6 52.4 %shard_map.59 = f32[32,128]{1,0:T(8,128)S(1)} custom-call(bf16[64,2048]{1,0:T(8,128)(2,1)} %test_hbm.1, bf16[64,4096]{1,0:T(8,128)(2,1)} %train_hbm.1, bf16[32,128]{1,0:T(8,128)(2,1)} %bitcast.5, bf16[4096,512]{1,0:T(8,128)(2,1)} %factor_hbm.1), custom_call_target="tpu_custom_call" | custom-call | tf_op jit(solution)/shard_map/pallas_call | solution.py:562
  53.1 0.6 %slice_bitcast_fusion = (f32[2048]{0:T(1024)}, f32[2048]{0:T(1024)}) fusion(f32[32,128]{1,0:T(8,128)S(1)} %shard_map.59), kind=kLoop, calls=%fused_computation | loop fusion | bytes 32768 | tf_op jit(solution)/shard_map/reshape | solution.py:588
